TPU v7x, 8 devices: a whole 2x2x1 slice. The times are simulated.
8 devices in a mesh: rep: 2 (over y, z), dp: 4 (over x, core).
Axes of the slice: x: 2, y: 2, z: 1, core: 2. Of those that a mesh axis runs over, the one named last changes fastest.
Arguments:
- g_w_gate: bfloat16 [8, 2, 1024, 3584], P(('rep', 'dp')), parts along dimension 0
- g_w_up: bfloat16 [8, 2, 1024, 3584], P(('rep', 'dp')), parts along dimension 0
- g_w_down: bfloat16 [8, 2, 3584, 1024], P(('rep', 'dp')), parts along dimension 0
- w_gate: bfloat16 [2, 1024, 3584], replicated
- w_up: bfloat16 [2, 1024, 3584], replicated
- w_down: bfloat16 [2, 3584, 1024], replicated
- m_w_gate: float32 [2, 1024, 3584], P(None, 'dp')
- m_w_up: float32 [2, 1024, 3584], P(None, 'dp')
- m_w_down: float32 [2, 3584, 1024], P(None, 'dp')
- v_w_gate: float32 [2, 1024, 3584], P(None, 'dp')
- v_w_up: float32 [2, 1024, 3584], P(None, 'dp')
- v_w_down: float32 [2, 3584, 1024], P(None, 'dp')
Outputs:
- output 1: bfloat16 [4, 1024, 3584], P('rep'), parts along dimension 0
- output 2: bfloat16 [4, 1024, 3584], P('rep'), parts along dimension 0
- output 3: bfloat16 [4, 3584, 1024], P('rep'), parts along dimension 0
- output 4: float32 [4, 1024, 3584], P('rep', 'dp'), parts along dimension 0
- output 5: float32 [4, 1024, 3584], P('rep', 'dp'), parts along dimension 0
- output 6: float32 [4, 3584, 1024], P('rep', 'dp'), parts along dimension 0
- output 7: float32 [4, 1024, 3584], P('rep', 'dp'), parts along dimension 0
- output 8: float32 [4, 1024, 3584], P('rep', 'dp'), parts along dimension 0
- output 9: float32 [4, 3584, 1024], P('rep', 'dp'), parts along dimension 0
There are 2 independent parts. A program takes and returns all parts, laid end to end along the dimension named above; an argument that names none is the same for every part.
All inputs are finite; a program needn't handle non-finite values.
Results may differ from a plain program's by a relative error of at most 0.022.
Values are sent between devices in bfloat16 or wider.
A program may use at most 2 GiB of HBM per device.

v0:
```python
import jax
import jax.numpy as jnp
from jax import lax
from jax.sharding import PartitionSpec as P


def adamw(w, m, v, g):
    m = 0.9 * m + 0.1 * g
    v = 0.95 * v + 0.05 * g * g
    step = m * lax.rsqrt(v + 1e-8) + 0.1 * w
    return (w - 0.02 * step).astype(jnp.bfloat16), m, v


def solution(mesh):
    def step(*arrays):
        terms, weights, m, v = (arrays[i : i + 3] for i in (0, 3, 6, 9))
        gradients = [lax.psum_scatter(t[0], "dp", scatter_dimension=1, tiled=True).astype(jnp.float32) for t in terms]
        me = lax.axis_index("dp")
        own = [lax.dynamic_slice_in_dim(w, me * one.shape[1], one.shape[1], 1).astype(jnp.float32) for w, one in zip(weights, m, strict=True)]
        new = [adamw(w, m, v, g) for w, m, v, g in zip(own, m, v, gradients, strict=True)]
        whole = [lax.all_gather(one[0], "dp", axis=1, tiled=True) for one in new]
        return (*whole, *(one[1] for one in new), *(one[2] for one in new))

    all_of, cut = P(None, None, None), P(None, "dp", None)
    return jax.shard_map(
        step,
        mesh=mesh,
        in_specs=(P(("rep", "dp"), None, None, None),) * 3 + (all_of,) * 3 + (cut,) * 6,
        out_specs=(P("rep", None, None),) * 3 + (P("rep", "dp", None),) * 6,
        check_vma=False,
    )
```

profile of v0, /device:TPU:0, one launch (start us, length us, event | category | flops | bytes accessed | tf_op | source)
XLA Modules:
  0.0 660.3 jit_solution(704478527384575817)
XLA Ops:
  7.2 0.0 reduce-scatter.8.cloned.1.call-start
  7.2 0.7 reduce-scatter.8.cloned.1.call-update
  7.9 0.0 reduce-scatter.6.cloned.1.call-start
  8.0 0.7 reduce-scatter.6.cloned.1.call-update
  8.7 0.0 reduce-scatter.4.cloned.1.call-start
  8.7 0.7 reduce-scatter.4.cloned.1.call-update
  9.4 0.0 all-gather.8.cloned.1.call-start
  9.4 112.3 %reduce-scatter.8.cloned.1.call-done = bf16[2,896,1024]{2,1,0:T(8,128)(2,1)} async-done(((bf16[2,3584,1024]{2,1,0:T(8,128)(2,1)}), bf16[2,896,1024]{2,1,0:T(8,128)(2,1)}) %reduce-scatter.8.cloned.1.call-update) | async-done | bytes 3670032 | tf_op jit(solution)/shard_map/reduce_scatter | solution.py:17
  121.8 18.5 %fusion.10 = (bf16[2,896,1024]{2,1,0:T(8,128)(2,1)}, f32[2,896,1024]{2,1,0:T(8,128)}, f32[2,896,1024]{2,1,0:T(8,128)}) fusion(bf16[2,3584,1024]{2,1,0:T(8,128)(2,1)} %param.17, s32[]{:T(128)S(6)} %select_n.8, bf16[2,896,1024]{2,1,0:T(8,128)(2,1)} %reduce-scatter.8.cloned.1.call-done, f32[2,896,1024]{2,1,0:T(8,128)} %param.23, f32[2,896,1024]{2,1,0:T(8,128)} %param.20), kind=kLoop, calls=%fused_computation.22 | loop fusion | flops 29360128 | bytes 40370180 | tf_op jit(solution)/shard_map/convert_element_type | solution.py:11
  140.2 0.0 all-gather.8.cloned.1.call-update
  140.3 0.0 all-gather.6.cloned.1.call-start
  140.3 92.5 %reduce-scatter.6.cloned.1.call-done = bf16[2,256,3584]{2,1,0:T(8,128)(2,1)} async-done(((bf16[2,1024,3584]{2,1,0:T(8,128)(2,1)}), bf16[2,256,3584]{2,1,0:T(8,128)(2,1)}) %reduce-scatter.6.cloned.1.call-update) | async-done | bytes 3670032 | tf_op jit(solution)/shard_map/reduce_scatter | solution.py:17
  232.8 18.3 %fusion.6 = (bf16[2,256,3584]{2,1,0:T(8,128)(2,1)}, f32[2,256,3584]{2,1,0:T(8,128)}, f32[2,256,3584]{2,1,0:T(8,128)}) fusion(bf16[2,1024,3584]{2,1,0:T(8,128)(2,1)} %param.16, s32[]{:T(128)S(6)} %select_n.7, bf16[2,256,3584]{2,1,0:T(8,128)(2,1)} %reduce-scatter.6.cloned.1.call-done, f32[2,256,3584]{2,1,0:T(8,128)} %param.22, f32[2,256,3584]{2,1,0:T(8,128)} %param.19), kind=kLoop, calls=%fused_computation.18 | loop fusion | flops 29360128 | bytes 40370180 | tf_op jit(solution)/shard_map/convert_element_type | solution.py:11
  251.1 0.0 all-gather.6.cloned.1.call-update
  251.1 0.0 all-gather.4.cloned.1.call-start
  251.2 92.6 %reduce-scatter.4.cloned.1.call-done = bf16[2,256,3584]{2,1,0:T(8,128)(2,1)} async-done(((bf16[2,1024,3584]{2,1,0:T(8,128)(2,1)}), bf16[2,256,3584]{2,1,0:T(8,128)(2,1)}) %reduce-scatter.4.cloned.1.call-update) | async-done | bytes 3670032 | tf_op jit(solution)/shard_map/reduce_scatter | solution.py:17
  343.8 17.0 %fusion.2 = (bf16[2,256,3584]{2,1,0:T(8,128)(2,1)}, f32[2,256,3584]{2,1,0:T(8,128)}, f32[2,256,3584]{2,1,0:T(8,128)}) fusion(bf16[2,1024,3584]{2,1,0:T(8,128)(2,1)} %param.15, s32[]{:T(128)S(6)} %select_n.7, bf16[2,256,3584]{2,1,0:T(8,128)(2,1)} %reduce-scatter.4.cloned.1.call-done, f32[2,256,3584]{2,1,0:T(8,128)} %param.21, f32[2,256,3584]{2,1,0:T(8,128)} %param.18), kind=kLoop, calls=%fused_computation.14 | loop fusion | flops 29360128 | bytes 40370180 | tf_op jit(solution)/shard_map/convert_element_type | solution.py:11
  360.8 0.0 all-gather.4.cloned.1.call-update
  360.8 76.2 %all-gather.8.cloned.1.call-done = bf16[2,3584,1024]{2,1,0:T(8,128)(2,1)} async-done(((bf16[2,896,1024]{2,1,0:T(8,128)(2,1)}), bf16[2,3584,1024]{2,1,0:T(8,128)(2,1)}) %all-gather.8.cloned.1.call-update) | async-done | bytes 14680080 | tf_op jit(solution)/shard_map/all_gather | solution.py:21
  437.0 93.2 %all-gather.6.cloned.1.call-done = bf16[2,1024,3584]{2,1,0:T(8,128)(2,1)} async-done(((bf16[2,256,3584]{2,1,0:T(8,128)(2,1)}), bf16[2,1024,3584]{2,1,0:T(8,128)(2,1)}) %all-gather.6.cloned.1.call-update) | async-done | bytes 14680080 | tf_op jit(solution)/shard_map/all_gather | solution.py:21
  530.2 93.2 %all-gather.4.cloned.1.call-done = bf16[2,1024,3584]{2,1,0:T(8,128)(2,1)} async-done(((bf16[2,256,3584]{2,1,0:T(8,128)(2,1)}), bf16[2,1024,3584]{2,1,0:T(8,128)(2,1)}) %all-gather.4.cloned.1.call-update) | async-done | bytes 14680080 | tf_op jit(solution)/shard_map/all_gather | solution.py:21
  623.4 0.0 copy-start
  623.4 0.0 slice-start
  623.4 0.0 slice-start.1
  623.4 15.7 %copy.24 = bf16[2,1024,3584]{2,1,0:T(8,128)(2,1)} copy(bf16[2,1024,3584]{2,1,0:T(8,128)(2,1)} %all-gather.4.cloned.1.call-done) | data formatting | bytes 29360128
  639.1 0.0 copy-done
  639.1 0.0 slice-start.2
  639.1 0.0 slice-start.3
  639.1 7.4 %copy.25 = bf16[2,1024,3584]{2,1,0:T(8,128)(2,1)} copy(bf16[2,1024,3584]{2,1,0:T(8,128)(2,1)S(1)} %copy-done) | data formatting | bytes 29360128
  646.6 0.0 slice-done
  646.6 0.0 slice-done.1
  646.6 0.1 slice-done.2
  646.7 1.3 slice-done.3
  648.0 5.5 copy.26
  (1 shorter events, 0.0 us)
Async XLA Ops:
  7.2 114.6 %reduce-scatter.8.cloned.1.call-start = ((), (), s32[]{:S(2)}) async-start(), calls=%async_computation.7 | async-start | bytes 18350080 | tf_op jit(solution)/shard_map/reduce_scatter | solution.py:17
  7.9 224.9 %reduce-scatter.6.cloned.1.call-start = ((), (), s32[]{:S(2)}) async-start(), calls=%async_computation.5 | async-start | bytes 18350080 | tf_op jit(solution)/shard_map/reduce_scatter | solution.py:17
  8.7 335.1 %reduce-scatter.4.cloned.1.call-start = ((), (), s32[]{:S(2)}) async-start(), calls=%async_computation.3 | async-start | bytes 18350080 | tf_op jit(solution)/shard_map/reduce_scatter | solution.py:17
  9.4 427.6 %all-gather.8.cloned.1.call-start = ((), (), s32[]{:S(2)}) async-start(), calls=%async_computation.8 | async-start | bytes 18350080 | tf_op jit(solution)/shard_map/all_gather | solution.py:21
  140.3 389.9 %all-gather.6.cloned.1.call-start = ((), (), s32[]{:S(2)}) async-start(), calls=%async_computation.6 | async-start | bytes 18350080 | tf_op jit(solution)/shard_map/all_gather | solution.py:21
  251.1 372.3 %all-gather.4.cloned.1.call-start = ((), (), s32[]{:S(2)}) async-start(), calls=%async_computation.4 | async-start | bytes 18350080 | tf_op jit(solution)/shard_map/all_gather | solution.py:21
  623.4 15.7 %copy-start = (bf16[2,1024,3584]{2,1,0:T(8,128)(2,1)S(1)}, bf16[2,1024,3584]{2,1,0:T(8,128)(2,1)}, u32[]{:S(2)}) copy-start(bf16[2,1024,3584]{2,1,0:T(8,128)(2,1)} %all-gather.6.cloned.1.call-done) | copy-start | bytes 44040196
  623.4 23.2 %slice-start = ((s8[14680064]{0:T(1024)(128)(4,1)}), s8[4194304]{0:T(1024)(128)(4,1)S(1)}, s32[]{:S(2)}) async-start(s8[14680064]{0:T(1024)(128)(4,1)} %bitcast.6), calls=%async_computation.9 | async-start | bytes 8388608
  623.4 23.2 %slice-start.1 = ((s8[14680064]{0:T(1024)(128)(4,1)}), s8[4194304]{0:T(1024)(128)(4,1)S(1)}, s32[]{:S(2)}) async-start(s8[14680064]{0:T(1024)(128)(4,1)} %bitcast.6), calls=%async_computation.10 | async-start | bytes 8388608
  639.1 7.6 %slice-start.2 = ((s8[14680064]{0:T(1024)(128)(4,1)}), s8[4194304]{0:T(1024)(128)(4,1)S(1)}, s32[]{:S(2)}) async-start(s8[14680064]{0:T(1024)(128)(4,1)} %bitcast.6), calls=%async_computation.11 | async-start | bytes 8388608
  639.1 8.9 %slice-start.3 = ((s8[14680064]{0:T(1024)(128)(4,1)}), s8[2097152]{0:T(1024)(128)(4,1)S(1)}, s32[]{:S(2)}) async-start(s8[14680064]{0:T(1024)(128)(4,1)} %bitcast.6), calls=%async_computation.12 | async-start | bytes 4194304
Sparse Core Ops, SparseCore 0:
  10.5 111.1 reduce-scatter.7
  124.3 108.4 reduce-scatter.5
  235.3 108.4 reduce-scatter.3
  345.8 91.2 all-gather.7
  439.0 91.1 all-gather.5
  532.2 91.1 all-gather.3
where the time goes:
time: 660 us
  waiting for transfers between devices  562 us (85%)
  other arithmetic  53.7 us (8%)
  local copies, waits for them, and re-layouts  30.1 us (5%)
  between operations  14.1 us (2%)
    reduce_scatter x3, waiting for transfers between devices, step(): lax.psum_scatter(t[0], 'dp', scatter_dimension=1, tiled=True)  297 us
    all_gather x3, waiting for transfers between devices, step(): whole = [lax.all_gather(one[0], 'dp', axis=1, tiled=True) for one in new]  263 us
    convert_element_type x3, other arithmetic, adamw(): return ((w - 0.02 * step).astype(jnp.bfloat16), m, v)  53.7 us
    unnamed x13, local copies, waits for them, and re-layouts  30.1 us
  transfers between devices with their start and end apart: 6, of which 6 were waited for; matrix products, arithmetic and copies ran while one was open for 8% of the time, Pallas kernels for 0%

commit v1 on v0

v1 whole, which is shorter than its diff:
```python
import jax
import jax.numpy as jnp
from jax import lax
from jax.experimental import pallas as pl
from jax.experimental.pallas import tpu as pltpu
from jax.sharding import PartitionSpec as P


CORES = [(0, 1), (1, 0), (2, 3), (3, 2)]
CHIPS = [(0, 2), (2, 0), (1, 3), (3, 1)]

FIRST = ((0, 0, 64), (0, 64, 192), (1, 0, 256))
LAST = ((0, 0, 896), (1, 0, 512), (1, 512, 256), (1, 768, 128))


def partners():
    me = lax.axis_index("dp")
    return me, me + 1 - 2 * (me % 2), (me + 2) % 4, 3 - me


def adamw(w, m, v, g):
    m = 0.9 * m + 0.1 * g
    v = 0.95 * v + 0.05 * g * g
    step = m * lax.rsqrt(v + 1e-8) + 0.1 * w
    return (w - 0.02 * step).astype(jnp.bfloat16), m, v


def place(shape, block, items, out=None):
    arrays = [one[0] for one in items]
    n = len(items)
    more = () if out is None else (out,)

    def kernel(*refs):
        pieces, refs = refs[:n], refs[n + len(more) :]
        whole, buffers, (read, wrote) = refs[0], refs[1 : 1 + n], refs[1 + n :]
        owners = partners()
        takes = [pltpu.make_async_copy(pieces[i], buffers[i], read.at[i]) for i in range(n)]
        for take in takes:
            take.start()
        puts = []
        for i, (array, who, layer, first) in enumerate(items):
            rows = pl.ds(pl.multiple_of(owners[who] * block + first, 16), array.shape[-2])
            put = pltpu.make_async_copy(buffers[i], whole.at[layer, rows] if array.ndim == 2 else whole.at[:, rows], wrote.at[i])
            takes[i].wait()
            put.start()
            puts.append(put)
        for put in puts:
            put.wait()

    size = sum(a.size for a in arrays)
    anywhere = pl.BlockSpec(memory_space=pltpu.HBM)
    return pl.pallas_call(
        kernel,
        out_shape=jax.ShapeDtypeStruct(shape, jnp.bfloat16),
        in_specs=[anywhere] * (n + len(more)),
        out_specs=anywhere,
        scratch_shapes=[pltpu.VMEM(a.shape, a.dtype) for a in arrays] + [pltpu.SemaphoreType.DMA((n,))] * 2,
        input_output_aliases={} if out is None else {n: 0},
        cost_estimate=pl.CostEstimate(flops=size * 8, bytes_accessed=4 * size, transcendentals=0),
        name="place",
    )(*arrays, *more)


def solution(mesh):
    def step(*arrays):
        terms, weights, ms, vs = (arrays[i : i + 3] for i in (0, 3, 6, 9))
        me, core, chip, both = partners()
        f32 = jnp.float32

        def part(array, who, piece, block):
            if piece is None:
                return lax.dynamic_slice_in_dim(array[0], who * block, block, 1)
            layer, first, rows = piece
            at = (0, layer, who * block + first, 0)
            return lax.dynamic_slice(array, at, (1, 1, rows, array.shape[-1])).reshape(rows, array.shape[-1])

        def send(array, pairs):
            return lax.ppermute(array, "dp", pairs)

        gate, up, down = terms
        far = []
        for n, piece in (*((0, piece) for piece in FIRST), (1, None), (2, None)):
            block = ms[n].shape[1]
            mine = part(terms[n], both, piece, block)
            theirs = send(mine, CORES)
            total = (part(terms[n], chip, piece, block).astype(f32) + theirs.astype(f32)).astype(jnp.bfloat16)
            far.append(send(total, CHIPS))
        far = [jnp.concatenate(far[:3], 0).reshape(ms[0].shape), *far[3:]]
        near = []
        for term, m in zip(terms, ms, strict=True):
            theirs = part(lax.optimization_barrier((term, total))[0], core, None, m.shape[1])
            near.append(send(theirs, CORES))

        new, wholes = [], []
        for term, w, m, v, other, beside, n in zip(terms, weights, ms, vs, far, near, range(3), strict=True):
            block = m.shape[1]
            own = part(term, me, None, block)
            g = lax.reduce_precision(own.astype(f32) + beside.astype(f32) + other.astype(f32), 8, 7)
            new.append(adamw(lax.dynamic_slice_in_dim(w, me * block, block, 1).astype(f32), m, v, g))
            out = new[-1][0]
            across = [send(out, CHIPS)] if n < 2 else []
            beside = send(out, CORES)
            whole = place(w.shape, block, [(out, 0, slice(None), 0), (beside, 1, slice(None), 0)])
            if n < 2:
                items = [(across[0], 2, slice(None), 0), (send(across[0], CORES), 3, slice(None), 0)]
                whole = place(w.shape, block, items, whole)
            else:
                for layer, row, rows in LAST:
                    across = send(out[layer, row : row + rows], CHIPS)
                    items = [(across, 2, layer, row), (send(across, CORES), 3, layer, row)]
                    whole = place(w.shape, block, items, whole)
            wholes.append(whole)
        return (*wholes, *(one[1] for one in new), *(one[2] for one in new))

    all_of, cut = P(None, None, None), P(None, "dp", None)
    return jax.shard_map(
        step,
        mesh=mesh,
        in_specs=(P(("rep", "dp"), None, None, None),) * 3 + (all_of,) * 3 + (cut,) * 6,
        out_specs=(P("rep", None, None),) * 3 + (P("rep", "dp", None),) * 6,
        check_vma=False,
    )
```

time: 660 us -> 555 us (0.84)
  waiting for transfers between devices: 562 us -> 398 us
  Pallas kernels: 0 us -> 36.1 us
  starting transfers between devices: 0.24 us -> 17 us
  other arithmetic: 53.7 us -> 70.3 us
  between operations: 14.1 us -> 1.09 us
    ppermute x0 -> x28, waiting for transfers between devices: none -> 398 us  [send(): return lax.ppermute(array, 'dp', pairs)]
    reduce_scatter x3 -> x0, waiting for transfers between devices: 297 us -> none  [step(): lax.psum_scatter(t[0], 'dp', scatter_dimension=1, tiled=True)]
    all_gather x3 -> x0, waiting for transfers between devices: 263 us -> none  [step(): whole = [lax.all_gather(one[0], 'dp', axis=1, tiled=True) for one in new]]
    pallas_call x0 -> x9, Pallas kernels: none -> 36.1 us  [place(): pl.pallas_call(kernel, out_shape=jax.ShapeDtypeStruct(shape, jnp.bfloat16...]
    unnamed x13 -> x26, local copies, waits for them, and re-layouts: 30.1 us -> 6.05 us
    dynamic_slice x0 -> x5, local copies, waits for them, and re-layouts: none -> 19 us  [part(): return lax.dynamic_slice_in_dim(array[0], who * block, block, 1)]
    convert_element_type x0 -> x5, other arithmetic: none -> 17.3 us  [step(): (part(terms[n], chip, piece, block).astype(f32) + theirs.astype(f32)).ast...]
    ppermute x0 -> x28, starting transfers between devices: none -> 17 us  [send(): return lax.ppermute(array, 'dp', pairs)]
  transfers between devices with their start and end apart: 6 -> 28, of which waited for: 6 -> 8; matrix products, arithmetic and copies ran while one was open for 8% -> 17% of each run, Pallas kernels for 0% -> 6%
where the time goes in v1:
time: 555 us
  waiting for transfers between devices  398 us (72%)
  other arithmetic  70.3 us (13%)
  Pallas kernels  36.1 us (7%)
  local copies, waits for them, and re-layouts  32.7 us (6%)
  starting transfers between devices  17 us (3%)
    ppermute x28, waiting for transfers between devices, send(): return lax.ppermute(array, 'dp', pairs)  398 us
    convert_element_type x3, other arithmetic, adamw(): return ((w - 0.02 * step).astype(jnp.bfloat16), m, v)  50.8 us
    pallas_call x9, Pallas kernels, place(): pl.pallas_call(kernel, out_shape=jax.ShapeDtypeStruct(shape, jnp.bfloat16...  36.1 us
    dynamic_slice x5, local copies, waits for them, and re-layouts, part(): return lax.dynamic_slice_in_dim(array[0], who * block, block, 1)  19 us
    convert_element_type x5, other arithmetic, step(): (part(terms[n], chip, piece, block).astype(f32) + theirs.astype(f32)).ast...  17.3 us
    ppermute x28, starting transfers between devices, send(): return lax.ppermute(array, 'dp', pairs)  17 us
  transfers between devices with their start and end apart: 28, of which 8 were waited for; matrix products, arithmetic and copies ran while one was open for 17% of the time, Pallas kernels for 6%

profile of v1, /device:TPU:0, one launch (start us, length us, event | category | flops | bytes accessed | tf_op | source)
XLA Modules:
  0.0 554.8 jit_solution(12593462912779164228)
XLA Ops:
  0.6 4.3 dynamic-slice_bitcast_fusion.4
  4.9 0.8 collective-permute-start
  5.7 1.8 dynamic-slice_bitcast_fusion.7
  7.6 1.4 dynamic-slice_bitcast_fusion.6
  9.0 0.5 collective-permute-start.4
  9.5 2.8 dynamic-slice_bitcast_fusion.5
  12.4 4.1 dynamic-slice_bitcast_fusion.1
  17.0 2.0 fusion.21
  19.0 2.5 collective-permute-start.3
  21.5 2.1 fusion.20
  23.6 5.2 fusion.18
  28.9 4.4 dynamic-slice_bitcast_fusion
  33.5 3.3 fusion.19
  36.8 1.7 collective-permute-start.7
  38.5 4.1 dynamic-slice_bitcast_fusion.3
  43.0 2.1 dynamic-slice_bitcast_fusion.2
  45.1 4.8 fusion.14
  49.8 130.5 %collective-permute-done.5 = bf16[192,3584]{1,0:T(8,128)(2,1)S(1)} collective-permute-done((bf16[192,3584]{1,0:T(8,128)(2,1)S(1)}, bf16[192,3584]{1,0:T(8,128)(2,1)S(1)}, u32[]{:S(2)}, u32[]{:S(2)}) %collective-permute-start.5) | collective-permute-done | bytes 1376288 | tf_op jit(solution)/shard_map/ppermute | solution.py:78
  180.4 1.1 copy-done.5
  181.4 1.2 copy-done.3
  182.7 1.7 collective-permute-start.13
  184.4 2.1 pad_maximum_fusion
  186.6 1.8 copy-done.1
  188.4 16.3 %fusion.8 = (bf16[2,896,1024]{2,1,0:T(8,128)(2,1)S(1)}, f32[2,896,1024]{2,1,0:T(8,128)}, f32[2,896,1024]{2,1,0:T(8,128)}) fusion(bf16[2,3584,1024]{2,1,0:T(8,128)(2,1)} %param.17, s32[]{:T(128)S(6)} %select_n.60, bf16[2,896,1024]{2,1,0:T(8,128)(2,1)} %collective-permute-done.18, bf16[2,896,1024]{2,1,0:T(8,128)(2,1)} %copy-done.1, ...), kind=kLoop, calls=%fused_computation.17 | loop fusion | flops 38535168 | bytes 47710212 | tf_op jit(solution)/shard_map/convert_element_type | solution.py:25
  204.7 1.5 slice_bitcast_fusion
  206.5 16.8 %fusion.2 = (bf16[2,256,3584]{2,1,0:T(8,128)(2,1)}, f32[2,256,3584]{2,1,0:T(8,128)}, f32[2,256,3584]{2,1,0:T(8,128)}) fusion(bf16[2,1024,3584]{2,1,0:T(8,128)(2,1)} %param.15, s32[]{:T(128)S(6)} %select_n.50, bf16[2,256,3584]{2,1,0:T(8,128)(2,1)S(1)} %bitcast.59, bf16[2,256,3584]{2,1,0:T(8,128)(2,1)} %collective-permute-done.1, ...), kind=kLoop, calls=%fused_computation.11 | loop fusion | flops 38535168 | bytes 47710212 | tf_op jit(solution)/shard_map/convert_element_type | solution.py:25
  223.2 1.7 collective-permute-start.8
  224.9 40.2 %collective-permute-done.13 = bf16[2,256,3584]{2,1,0:T(8,128)(2,1)} collective-permute-done((bf16[2,256,3584]{2,1,0:T(8,128)(2,1)}, bf16[2,256,3584]{2,1,0:T(8,128)(2,1)}, u32[]{:S(2)}, u32[]{:S(2)}) %collective-permute-start.13) | collective-permute-done | bytes 3670048 | tf_op jit(solution)/shard_map/ppermute | solution.py:78
  265.2 17.8 %fusion.5 = (bf16[2,256,3584]{2,1,0:T(8,128)(2,1)}, f32[2,256,3584]{2,1,0:T(8,128)}, f32[2,256,3584]{2,1,0:T(8,128)}) fusion(bf16[2,1024,3584]{2,1,0:T(8,128)(2,1)} %param.16, s32[]{:T(128)S(6)} %select_n.50, bf16[2,256,3584]{2,1,0:T(8,128)(2,1)} %collective-permute-done.13, bf16[2,256,3584]{2,1,0:T(8,128)(2,1)} %collective-permute-done.11, ...), kind=kLoop, calls=%fused_computation.14 | loop fusion | flops 38535168 | bytes 47710212 | tf_op jit(solution)/shard_map/convert_element_type | solution.py:25
  283.0 1.7 collective-permute-start.14
  285.1 19.4 %collective-permute-done.25.refs_0_ = bf16[896,1024]{1,0:T(8,128)(2,1)} collective-permute-done((bf16[896,1024]{1,0:T(8,128)(2,1)}, bf16[896,1024]{1,0:T(8,128)(2,1)}, u32[]{:S(2)}, u32[]{:S(2)}) %collective-permute-start.25) | collective-permute-done | bytes 1835040 | tf_op jit(solution)/shard_map/ppermute | solution.py:78
  304.5 1.8 collective-permute-start.19
  306.3 182.5 %collective-permute-done.19.refs_0_ = bf16[128,1024]{1,0:T(8,128)(2,1)} collective-permute-done((bf16[128,1024]{1,0:T(8,128)(2,1)S(1)}, bf16[128,1024]{1,0:T(8,128)(2,1)}, u32[]{:S(2)}, u32[]{:S(2)}) %collective-permute-start.19) | collective-permute-done | bytes 262176 | tf_op jit(solution)/shard_map/ppermute | solution.py:78
  488.8 1.5 collective-permute-start.21
  490.3 11.4 %collective-permute-done.21.refs_0_ = bf16[256,1024]{1,0:T(8,128)(2,1)S(1)} collective-permute-done((bf16[256,1024]{1,0:T(8,128)(2,1)S(1)}, bf16[256,1024]{1,0:T(8,128)(2,1)S(1)}, u32[]{:S(2)}, u32[]{:S(2)}) %collective-permute-start.21) | collective-permute-done | bytes 524320 | tf_op jit(solution)/shard_map/ppermute | solution.py:78
  501.7 2.0 collective-permute-done.22.refs_1_
  505.0 5.2 collective-permute-done.27.refs_1_
  510.2 1.9 copy-done.2
  512.2 5.3 place.13.refs_2_
  517.5 3.4 place.14.refs_2_
  520.9 2.6 place.15.refs_2_
  523.5 2.0 place.16.refs_2_
  525.5 6.2 %collective-permute-done.20.refs_1_ = bf16[128,1024]{1,0:T(8,128)(2,1)} collective-permute-done((bf16[128,1024]{1,0:T(8,128)(2,1)}, bf16[128,1024]{1,0:T(8,128)(2,1)}, u32[]{:S(2)}, u32[]{:S(2)}) %collective-permute-start.20) | collective-permute-done | bytes 262176 | tf_op jit(solution)/shard_map/ppermute | solution.py:78
  531.7 1.8 place.17
  533.5 5.3 place.9.refs_2_
  538.8 5.3 place.11.refs_2_
  544.0 5.3 place.10
  549.3 5.3 place.12
  (65 shorter events, 3.2 us)
Async XLA Ops:
  4.9 18.7 %collective-permute-start = (bf16[2,896,1024]{2,1,0:T(8,128)(2,1)}, bf16[2,896,1024]{2,1,0:T(8,128)(2,1)}, u32[]{:S(2)}, u32[]{:S(2)}) collective-permute-start(bf16[2,896,1024]{2,1,0:T(8,128)(2,1)} %dynamic-slice_bitcast_fusion.4), channel_id=1, source_target_pairs={{0,1},{1,0},{2,3},{3,2},{4,5},{5,4},{6,7},{7,6}} | collective-permute-start | bytes 11010056 | tf_op jit(solution)/shard_map/ppermute | solution.py:78
  7.6 9.4 %collective-permute-start.2 = (bf16[64,3584]{1,0:T(8,128)(2,1)}, bf16[64,3584]{1,0:T(8,128)(2,1)}, u32[]{:S(2)}, u32[]{:S(2)}) collective-permute-start(bf16[64,3584]{1,0:T(8,128)(2,1)} %dynamic-slice_bitcast_fusion.7), channel_id=1, source_target_pairs={{0,1},{1,0},{2,3},{3,2},{4,5},{5,4},{6,7},{7,6}} | collective-permute-start | bytes 1376264 | tf_op jit(solution)/shard_map/ppermute | solution.py:78
  9.0 12.5 %collective-permute-start.4 = (bf16[192,3584]{1,0:T(8,128)(2,1)S(1)}, bf16[192,3584]{1,0:T(8,128)(2,1)}, u32[]{:S(2)}, u32[]{:S(2)}) collective-permute-start(bf16[192,3584]{1,0:T(8,128)(2,1)S(1)} %dynamic-slice_bitcast_fusion.6), channel_id=1, source_target_pairs={{0,1},{1,0},{2,3},{3,2},{4,5},{5,4},{6,7},{7,6}} | collective-permute-start | bytes 4128776 | tf_op jit(solution)/shard_map/ppermute | solution.py:78
  12.4 21.2 %collective-permute-start.6 = (bf16[256,3584]{1,0:T(8,128)(2,1)}, bf16[256,3584]{1,0:T(8,128)(2,1)S(1)}, u32[]{:S(2)}, u32[]{:S(2)}) collective-permute-start(bf16[256,3584]{1,0:T(8,128)(2,1)} %dynamic-slice_bitcast_fusion.5), channel_id=1, source_target_pairs={{0,1},{1,0},{2,3},{3,2},{4,5},{5,4},{6,7},{7,6}} | collective-permute-start | bytes 5505032 | tf_op jit(solution)/shard_map/ppermute | solution.py:78
  16.5 26.5 %collective-permute-start.12 = (bf16[2,256,3584]{2,1,0:T(8,128)(2,1)}, bf16[2,256,3584]{2,1,0:T(8,128)(2,1)}, u32[]{:S(2)}, u32[]{:S(2)}) collective-permute-start(bf16[2,256,3584]{2,1,0:T(8,128)(2,1)} %dynamic-slice_bitcast_fusion.1), channel_id=1, source_target_pairs={{0,1},{1,0},{2,3},{3,2},{4,5},{5,4},{6,7},{7,6}} | collective-permute-start | bytes 11010056 | tf_op jit(solution)/shard_map/ppermute | solution.py:78
  19.0 23.6 %collective-permute-start.3 = (bf16[64,3584]{1,0:T(8,128)(2,1)}, bf16[64,3584]{1,0:T(8,128)(2,1)}, u32[]{:S(2)}, u32[]{:S(2)}) collective-permute-start(bf16[64,3584]{1,0:T(8,128)(2,1)} %fusion.21), channel_id=1, source_target_pairs={{0,2},{2,0},{1,3},{3,1},{4,6},{6,4},{5,7},{7,5}} | collective-permute-start | bytes 1376264 | tf_op jit(solution)/shard_map/ppermute | solution.py:78
  23.6 19.4 %slice-start = ((s8[14680064]{0:T(1024)(128)(4,1)}), s8[4194304]{0:T(1024)(128)(4,1)S(1)}, s32[]{:S(2)}) async-start(s8[14680064]{0:T(1024)(128)(4,1)} %bitcast.60), calls=%async_computation | async-start | bytes 8388608
  23.6 19.4 %slice-start.1 = ((s8[14680064]{0:T(1024)(128)(4,1)}), s8[4194304]{0:T(1024)(128)(4,1)S(1)}, s32[]{:S(2)}) async-start(s8[14680064]{0:T(1024)(128)(4,1)} %bitcast.60), calls=%async_computation.1 | async-start | bytes 8388608
  28.9 14.1 %slice-start.2 = ((s8[14680064]{0:T(1024)(128)(4,1)}), s8[4194304]{0:T(1024)(128)(4,1)S(1)}, s32[]{:S(2)}) async-start(s8[14680064]{0:T(1024)(128)(4,1)} %bitcast.60), calls=%async_computation.2 | async-start | bytes 8388608
  28.9 159.5 %collective-permute-start.18 = (bf16[2,896,1024]{2,1,0:T(8,128)(2,1)S(1)}, bf16[2,896,1024]{2,1,0:T(8,128)(2,1)}, u32[]{:S(2)}, u32[]{:S(2)}) collective-permute-start(bf16[2,896,1024]{2,1,0:T(8,128)(2,1)S(1)} %fusion.18), channel_id=1, source_target_pairs={{0,2},{2,0},{1,3},{3,1},{4,6},{6,4},{5,7},{7,5}} | collective-permute-start | bytes 11010056 | tf_op jit(solution)/shard_map/ppermute | solution.py:78
  33.3 9.7 %slice-start.3 = ((s8[14680064]{0:T(1024)(128)(4,1)}), s8[2097152]{0:T(1024)(128)(4,1)S(1)}, s32[]{:S(2)}) async-start(s8[14680064]{0:T(1024)(128)(4,1)} %bitcast.60), calls=%async_computation.3 | async-start | bytes 4194304
  33.3 153.2 %collective-permute-start.17 = (bf16[2,896,1024]{2,1,0:T(8,128)(2,1)}, bf16[2,896,1024]{2,1,0:T(8,128)(2,1)S(1)}, u32[]{:S(2)}, u32[]{:S(2)}) collective-permute-start(bf16[2,896,1024]{2,1,0:T(8,128)(2,1)} %dynamic-slice_bitcast_fusion), channel_id=1, source_target_pairs={{0,1},{1,0},{2,3},{3,2},{4,5},{5,4},{6,7},{7,6}} | collective-permute-start | bytes 11010056 | tf_op jit(solution)/shard_map/ppermute | solution.py:78
  36.8 143.6 %collective-permute-start.7 = (bf16[256,3584]{1,0:T(8,128)(2,1)}, bf16[256,3584]{1,0:T(8,128)(2,1)S(1)}, u32[]{:S(2)}, u32[]{:S(2)}) collective-permute-start(bf16[256,3584]{1,0:T(8,128)(2,1)} %fusion.19), channel_id=1, source_target_pairs={{0,2},{2,0},{1,3},{3,1},{4,6},{6,4},{5,7},{7,5}} | collective-permute-start | bytes 5505032 | tf_op jit(solution)/shard_map/ppermute | solution.py:78
  42.6 137.8 %collective-permute-start.5 = (bf16[192,3584]{1,0:T(8,128)(2,1)S(1)}, bf16[192,3584]{1,0:T(8,128)(2,1)S(1)}, u32[]{:S(2)}, u32[]{:S(2)}) collective-permute-start(bf16[192,3584]{1,0:T(8,128)(2,1)S(1)} %fusion.20), channel_id=1, source_target_pairs={{0,2},{2,0},{1,3},{3,1},{4,6},{6,4},{5,7},{7,5}} | collective-permute-start | bytes 4128776 | tf_op jit(solution)/shard_map/ppermute | solution.py:78
  43.0 163.5 %collective-permute-start.1 = (bf16[2,256,3584]{2,1,0:T(8,128)(2,1)}, bf16[2,256,3584]{2,1,0:T(8,128)(2,1)}, u32[]{:S(2)}, u32[]{:S(2)}) collective-permute-start(bf16[2,256,3584]{2,1,0:T(8,128)(2,1)} %dynamic-slice_bitcast_fusion.3), channel_id=1, source_target_pairs={{0,1},{1,0},{2,3},{3,2},{4,5},{5,4},{6,7},{7,6}} | collective-permute-start | bytes 11010056 | tf_op jit(solution)/shard_map/ppermute | solution.py:78
  180.4 1.1 copy-start.5
  180.4 44.6 %collective-permute-start.11 = (bf16[2,256,3584]{2,1,0:T(8,128)(2,1)}, bf16[2,256,3584]{2,1,0:T(8,128)(2,1)}, u32[]{:S(2)}, u32[]{:S(2)}) collective-permute-start(bf16[2,256,3584]{2,1,0:T(8,128)(2,1)} %dynamic-slice_bitcast_fusion.2), channel_id=1, source_target_pairs={{0,1},{1,0},{2,3},{3,2},{4,5},{5,4},{6,7},{7,6}} | collective-permute-start | bytes 11010056 | tf_op jit(solution)/shard_map/ppermute | solution.py:78
  181.4 1.2 copy-start.3
  182.7 82.5 %collective-permute-start.13 = (bf16[2,256,3584]{2,1,0:T(8,128)(2,1)}, bf16[2,256,3584]{2,1,0:T(8,128)(2,1)}, u32[]{:S(2)}, u32[]{:S(2)}) collective-permute-start(bf16[2,256,3584]{2,1,0:T(8,128)(2,1)} %fusion.14), channel_id=1, source_target_pairs={{0,2},{2,0},{1,3},{3,1},{4,6},{6,4},{5,7},{7,5}} | collective-permute-start | bytes 11010056 | tf_op jit(solution)/shard_map/ppermute | solution.py:78
  186.6 1.8 copy-start.1
  204.7 299.1 %copy-start = (bf16[2,896,1024]{2,1,0:T(8,128)(2,1)}, bf16[2,896,1024]{2,1,0:T(8,128)(2,1)S(1)}, u32[]{:S(2)}) copy-start(bf16[2,896,1024]{2,1,0:T(8,128)(2,1)S(1)} %get-tuple-element.15.refs_0_) | copy-start | bytes 11010052
  206.2 98.3 %collective-permute-start.25 = (bf16[896,1024]{1,0:T(8,128)(2,1)}, bf16[896,1024]{1,0:T(8,128)(2,1)}, u32[]{:S(2)}, u32[]{:S(2)}) collective-permute-start(bf16[896,1024]{1,0:T(8,128)(2,1)} %slice_bitcast_fusion), channel_id=1, source_target_pairs={{0,2},{2,0},{1,3},{3,1},{4,6},{6,4},{5,7},{7,5}} | collective-permute-start | bytes 5505032 | tf_op jit(solution)/shard_map/ppermute | solution.py:78
  223.2 281.2 %collective-permute-start.8 = (bf16[2,256,3584]{2,1,0:T(8,128)(2,1)}, bf16[2,256,3584]{2,1,0:T(8,128)(2,1)}, u32[]{:S(2)}, u32[]{:S(2)}) collective-permute-start(bf16[2,256,3584]{2,1,0:T(8,128)(2,1)} %get-tuple-element.21.refs_0_), channel_id=1, source_target_pairs={{0,2},{2,0},{1,3},{3,1},{4,6},{6,4},{5,7},{7,5}} | collective-permute-start | bytes 11010056 | tf_op jit(solution)/shard_map/ppermute | solution.py:78
  283.0 221.8 %collective-permute-start.14 = (bf16[2,256,3584]{2,1,0:T(8,128)(2,1)}, bf16[2,256,3584]{2,1,0:T(8,128)(2,1)}, u32[]{:S(2)}, u32[]{:S(2)}) collective-permute-start(bf16[2,256,3584]{2,1,0:T(8,128)(2,1)} %get-tuple-element.18.refs_0_), channel_id=1, source_target_pairs={{0,2},{2,0},{1,3},{3,1},{4,6},{6,4},{5,7},{7,5}} | collective-permute-start | bytes 11010056 | tf_op jit(solution)/shard_map/ppermute | solution.py:78
  284.8 205.5 %collective-permute-start.23 = (bf16[512,1024]{1,0:T(8,128)(2,1)S(1)}, bf16[512,1024]{1,0:T(8,128)(2,1)S(1)}, u32[]{:S(2)}, u32[]{:S(2)}) collective-permute-start(bf16[512,1024]{1,0:T(8,128)(2,1)S(1)} %slice_bitcast_fusion.1), channel_id=1, source_target_pairs={{0,2},{2,0},{1,3},{3,1},{4,6},{6,4},{5,7},{7,5}} | collective-permute-start | bytes 3145736 | tf_op jit(solution)/shard_map/ppermute | solution.py:78
  304.5 199.8 %collective-permute-start.26 = (bf16[896,1024]{1,0:T(8,128)(2,1)}, bf16[896,1024]{1,0:T(8,128)(2,1)S(1)}, u32[]{:S(2)}, u32[]{:S(2)}) collective-permute-start(bf16[896,1024]{1,0:T(8,128)(2,1)} %collective-permute-done.25.refs_0_), channel_id=1, source_target_pairs={{0,1},{1,0},{2,3},{3,2},{4,5},{5,4},{6,7},{7,6}} | collective-permute-start | bytes 5505032 | tf_op jit(solution)/shard_map/ppermute | solution.py:78
  304.5 184.3 %collective-permute-start.19 = (bf16[128,1024]{1,0:T(8,128)(2,1)S(1)}, bf16[128,1024]{1,0:T(8,128)(2,1)}, u32[]{:S(2)}, u32[]{:S(2)}) collective-permute-start(bf16[128,1024]{1,0:T(8,128)(2,1)S(1)} %slice_bitcast_fusion.3), channel_id=1, source_target_pairs={{0,2},{2,0},{1,3},{3,1},{4,6},{6,4},{5,7},{7,5}} | collective-permute-start | bytes 786440 | tf_op jit(solution)/shard_map/ppermute | solution.py:78
  488.8 12.9 %collective-permute-start.21 = (bf16[256,1024]{1,0:T(8,128)(2,1)S(1)}, bf16[256,1024]{1,0:T(8,128)(2,1)S(1)}, u32[]{:S(2)}, u32[]{:S(2)}) collective-permute-start(bf16[256,1024]{1,0:T(8,128)(2,1)S(1)} %slice_bitcast_fusion.2), channel_id=1, source_target_pairs={{0,2},{2,0},{1,3},{3,1},{4,6},{6,4},{5,7},{7,5}} | collective-permute-start | bytes 1572872 | tf_op jit(solution)/shard_map/ppermute | solution.py:78
  490.3 30.6 %copy-start.6 = (bf16[512,1024]{1,0:T(8,128)(2,1)}, bf16[512,1024]{1,0:T(8,128)(2,1)S(1)}, u32[]{:S(2)}) copy-start(bf16[512,1024]{1,0:T(8,128)(2,1)S(1)} %collective-permute-done.23.refs_0_) | copy-start | bytes 3145732
  490.3 13.6 %collective-permute-start.24 = (bf16[512,1024]{1,0:T(8,128)(2,1)S(1)}, bf16[512,1024]{1,0:T(8,128)(2,1)S(1)}, u32[]{:S(2)}, u32[]{:S(2)}) collective-permute-start(bf16[512,1024]{1,0:T(8,128)(2,1)S(1)} %collective-permute-done.23.refs_0_), channel_id=1, source_target_pairs={{0,1},{1,0},{2,3},{3,2},{4,5},{5,4},{6,7},{7,6}} | collective-permute-start | bytes 3145736 | tf_op jit(solution)/shard_map/ppermute | solution.py:78
  501.7 19.2 %copy-start.8 = (bf16[256,1024]{1,0:T(8,128)(2,1)}, bf16[256,1024]{1,0:T(8,128)(2,1)S(1)}, u32[]{:S(2)}) copy-start(bf16[256,1024]{1,0:T(8,128)(2,1)S(1)} %collective-permute-done.21.refs_0_) | copy-start | bytes 1572868
  501.7 2.0 collective-permute-start.22
  503.8 6.4 %collective-permute-start.27 = (bf16[2,896,1024]{2,1,0:T(8,128)(2,1)S(1)}, bf16[2,896,1024]{2,1,0:T(8,128)(2,1)S(1)}, u32[]{:S(2)}, u32[]{:S(2)}) collective-permute-start(bf16[2,896,1024]{2,1,0:T(8,128)(2,1)S(1)} %get-tuple-element.15.refs_0_), channel_id=1, source_target_pairs={{0,1},{1,0},{2,3},{3,2},{4,5},{5,4},{6,7},{7,6}} | collective-permute-start | bytes 11010056 | tf_op jit(solution)/shard_map/ppermute | solution.py:78
  503.9 6.3 %copy-start.7 = (bf16[512,1024]{1,0:T(8,128)(2,1)}, bf16[512,1024]{1,0:T(8,128)(2,1)S(1)}, u32[]{:S(2)}) copy-start(bf16[512,1024]{1,0:T(8,128)(2,1)S(1)} %collective-permute-done.24.refs_1_) | copy-start | bytes 3145732
  503.9 29.6 %collective-permute-start.10 = (bf16[2,256,3584]{2,1,0:T(8,128)(2,1)}, bf16[2,256,3584]{2,1,0:T(8,128)(2,1)}, u32[]{:S(2)}, u32[]{:S(2)}) collective-permute-start(bf16[2,256,3584]{2,1,0:T(8,128)(2,1)} %get-tuple-element.21.refs_0_), channel_id=1, source_target_pairs={{0,1},{1,0},{2,3},{3,2},{4,5},{5,4},{6,7},{7,6}} | collective-permute-start | bytes 11010056 | tf_op jit(solution)/shard_map/ppermute | solution.py:78
  504.3 13.2 %copy-start.4 = (bf16[896,1024]{1,0:T(8,128)(2,1)}, bf16[896,1024]{1,0:T(8,128)(2,1)S(1)}, u32[]{:S(2)}) copy-start(bf16[896,1024]{1,0:T(8,128)(2,1)S(1)} %collective-permute-done.26.refs_1_) | copy-start | bytes 5505028
  504.3 34.5 %collective-permute-start.16 = (bf16[2,256,3584]{2,1,0:T(8,128)(2,1)}, bf16[2,256,3584]{2,1,0:T(8,128)(2,1)}, u32[]{:S(2)}, u32[]{:S(2)}) collective-permute-start(bf16[2,256,3584]{2,1,0:T(8,128)(2,1)} %get-tuple-element.18.refs_0_), channel_id=1, source_target_pairs={{0,1},{1,0},{2,3},{3,2},{4,5},{5,4},{6,7},{7,6}} | collective-permute-start | bytes 11010056 | tf_op jit(solution)/shard_map/ppermute | solution.py:78
  504.4 39.6 %collective-permute-start.9 = (bf16[2,256,3584]{2,1,0:T(8,128)(2,1)}, bf16[2,256,3584]{2,1,0:T(8,128)(2,1)}, u32[]{:S(2)}, u32[]{:S(2)}) collective-permute-start(bf16[2,256,3584]{2,1,0:T(8,128)(2,1)} %collective-permute-done.8.refs_0_), channel_id=1, source_target_pairs={{0,1},{1,0},{2,3},{3,2},{4,5},{5,4},{6,7},{7,6}} | collective-permute-start | bytes 11010056 | tf_op jit(solution)/shard_map/ppermute | solution.py:78
  504.8 44.5 %collective-permute-start.15 = (bf16[2,256,3584]{2,1,0:T(8,128)(2,1)}, bf16[2,256,3584]{2,1,0:T(8,128)(2,1)}, u32[]{:S(2)}, u32[]{:S(2)}) collective-permute-start(bf16[2,256,3584]{2,1,0:T(8,128)(2,1)} %collective-permute-done.14.refs_0_), channel_id=1, source_target_pairs={{0,1},{1,0},{2,3},{3,2},{4,5},{5,4},{6,7},{7,6}} | collective-permute-start | bytes 11010056 | tf_op jit(solution)/shard_map/ppermute | solution.py:78
  510.2 1.9 copy-start.2
  512.1 19.6 %collective-permute-start.20 = (bf16[128,1024]{1,0:T(8,128)(2,1)}, bf16[128,1024]{1,0:T(8,128)(2,1)}, u32[]{:S(2)}, u32[]{:S(2)}) collective-permute-start(bf16[128,1024]{1,0:T(8,128)(2,1)} %collective-permute-done.19.refs_0_), channel_id=1, source_target_pairs={{0,1},{1,0},{2,3},{3,2},{4,5},{5,4},{6,7},{7,6}} | collective-permute-start | bytes 786440 | tf_op jit(solution)/shard_map/ppermute | solution.py:78
